TPU v7x, 32 devices: a whole 2x2x4 slice. The times are simulated.
32 devices in a mesh: rowa: 2 (over x), rowb: 4 (over z), col: 4 (over y, core).
Axes of the slice: x: 2, y: 2, z: 4, core: 2. Of those that a mesh axis runs over, the one named last changes fastest.
Arguments:
- table: float32 [65536, 512], P(('rowa', 'rowb'), 'col'), may hold values from -12 to 12
- start: float32 [16, 512], P(None, 'col'), may hold values from -6 to 6
Outputs:
- right_vectors: float32 [16, 512], P(None, 'col')
- left_images: float32 [16, 65536], P(None, ('rowa', 'rowb'))
- strengths: float32 [16], replicated
All inputs are finite; a program needn't handle non-finite values.
Results may differ from a plain program's by a relative error of at most 0.00014.
Values sent between devices are 32-bit elements.
A program may use at most 64 MiB of HBM per device.

v0:
```python
import jax
import jax.numpy as jnp
from jax import lax
from jax.sharding import PartitionSpec as P

STEPS = 8
high = lax.Precision.HIGHEST


def apply_rows(vectors, table):
    return lax.dot_general(
        vectors, table, (((1,), (1,)), ((), ())), precision=high, preferred_element_type=jnp.float32
    )


def outer_gram(products):
    return lax.dot_general(
        products,
        products,
        (((1,), (1,)), ((), ())),
        precision=high,
        preferred_element_type=jnp.float32,
    )


def normalize(gram, products):
    lower = jnp.linalg.cholesky(gram)
    return (jax.scipy.linalg.solve_triangular(lower, products, lower=True), lower)


def own_columns(vectors, start):
    width = start.shape[1]
    offset = lax.axis_index("col") * width
    return lax.dynamic_slice_in_dim(vectors, offset, width, 1)


def on_device(table, start):
    regrouped = lax.all_to_all(table, "col", split_axis=0, concat_axis=1, tiled=True)
    rows_total = table.shape[0] * lax.axis_size("rowa") * lax.axis_size("rowb")
    vectors = lax.all_gather(start, "col", axis=1, tiled=True)
    partial_cover = lax.dot_general(
        regrouped,
        regrouped,
        (((0,), (0,)), ((), ())),
        precision=high,
        preferred_element_type=jnp.float32,
    )
    cover = lax.psum(partial_cover, ("rowa", "rowb", "col"))
    previous = vectors
    lower = None
    for step in range(STEPS):
        previous = vectors
        products = jnp.dot(vectors, cover, precision=high, preferred_element_type=jnp.float32)
        vectors, lower = normalize(outer_gram(products), products)
    images = apply_rows(previous, regrouped)
    left = lax.all_gather(images, "col", axis=1, tiled=True)
    return (own_columns(vectors, start), left, jnp.diagonal(lower) / rows_total)


def solution(mesh):
    placed = (P(("rowa", "rowb"), "col"), P(None, "col"))
    return jax.shard_map(
        on_device,
        mesh=mesh,
        in_specs=placed,
        out_specs=(P(None, "col"), P(None, ("rowa", "rowb")), P()),
        check_vma=False,
    )
```

profile of v0, /device:TPU:0, one launch (start us, length us, event | category | flops | bytes accessed | tf_op | source)
XLA Modules:
  0.0 275.0 jit_solution(15089997109972043354)
XLA Ops:
  7.2 54.6 %all_to_all.19 = f32[4,2048,128]{2,1,0:T(8,128)} all-to-all(f32[4,2048,128]{2,1,0:T(8,128)} %bitcast.126), channel_id=1, replica_groups=mesh['rowa'=2,'rowb'=4,'col'=4] {'col'}, dimensions={0} | all-to-all | bytes 8388608 | tf_op jit(solution)/shard_map/all_to_all | solution.py:38
  61.8 5.4 %copy.21 = f32[2048,4,128]{0,2,1:T(8,128)} copy(f32[2048,4,128]{2,0,1:T(8,128)} %bitcast.125) | data formatting | bytes 8388608 | tf_op jit(solution)/shard_map/all_to_all | solution.py:38
  67.1 10.3 %fusion.48 = f32[512,512]{1,0:T(8,128)} fusion(f32[2048,512]{0,1:T(8,128)} %bitcast.123), kind=kOutput, calls=%fused_computation.78 | convolution fusion | flops 6442450944 | bytes 5242880 | tf_op jit(solution)/shard_map/dot_general | solution.py:41
  77.5 5.4 %all_gather.6 = f32[16,512]{1,0:T(8,128)S(1)} all-gather(f32[16,128]{1,0:T(8,128)S(1)} %copy-done.1), channel_id=1, replica_groups=mesh['rowa'=2,'rowb'=4,'col'=4] {'col'}, dimensions={1}, use_global_device_ids=true | all-gather | bytes 40960 | tf_op jit(solution)/shard_map/all_gather | solution.py:40
  82.9 126.5 %all-reduce.2.cloned.1.call-done = f32[512,512]{1,0:T(8,128)} async-done(((f32[512,512]{1,0:T(8,128)}), f32[512,512]{1,0:T(8,128)}) %all-reduce.2.cloned.1.call-update) | async-done | bytes 1048592 | tf_op jit(solution)/shard_map/psum | solution.py:48
  209.4 2.0 fusion.49
  211.6 1.5 cholesky.134
  214.4 1.2 custom-call.14
  215.8 1.9 fusion.51
  217.9 1.5 cholesky.145
  220.7 1.2 custom-call.15
  222.2 1.9 fusion.53
  224.3 1.5 cholesky.156
  227.1 1.2 custom-call.16
  229.4 1.5 cholesky.167
  232.2 1.2 custom-call.17
  234.6 1.5 cholesky.178
  237.4 1.2 custom-call.18
  239.7 1.5 cholesky.189
  244.8 1.5 cholesky.200
  249.1 4.3 %fusion.65 = f32[16,2048]{1,0:T(8,128)S(1)} fusion(f32[16,512]{1,0:T(8,128)S(1)} %fusion.12, f32[2048,512]{0,1:T(8,128)} %bitcast.124), kind=kOutput, calls=%fused_computation.95 | convolution fusion | flops 201326592 | bytes 4358144 | tf_op jit(solution)/shard_map/dot_general | solution.py:11
  253.4 7.1 %all_gather.7 = f32[16,8192]{1,0:T(8,128)S(1)} all-gather(f32[16,2048]{1,0:T(8,128)S(1)} %fusion.65), channel_id=1, replica_groups=mesh['rowa'=2,'rowb'=4,'col'=4] {'col'}, dimensions={1}, use_global_device_ids=true | all-gather | bytes 655360 | tf_op jit(solution)/shard_map/all_gather | solution.py:56
  261.3 1.5 cholesky.211
  264.1 1.2 custom-call.21
  (74 shorter events, 22.5 us)
Async XLA Ops:
  7.2 202.2 %all-reduce.2.cloned.1.call-start = ((), (), s32[]{:S(2)}) async-start(), calls=%async_computation.1 | async-start | bytes 2097152 | tf_op jit(solution)/shard_map/psum | solution.py:48
  67.1 10.4 %copy-start.1 = (f32[16,128]{1,0:T(8,128)S(1)}, f32[16,128]{1,0:T(8,128)}, u32[]{:S(2)}) copy-start(f32[16,128]{1,0:T(8,128)} %param.6) | copy-start | bytes 24580
  209.4 19.2 %copy-start = (f32[512,512]{1,0:T(8,128)S(1)}, f32[512,512]{1,0:T(8,128)}, u32[]{:S(2)}) copy-start(f32[512,512]{1,0:T(8,128)} %all-reduce.2.cloned.1.call-done) | copy-start | bytes 3145732
Sparse Core Ops, SparseCore 0:
  77.6 131.7 all-reduce.1
where the time goes:
time: 276 us; the launch traced here: 275 us
  waiting for transfers between devices  127 us (46%)
  blocking collectives  67 us (24%)
  other arithmetic  32.8 us (12%)
  matrix products  26.4 us (10%)
  between operations  14.2 us (5%)
  local copies, waits for them, and re-layouts  8.11 us (3%)
    psum x1, waiting for transfers between devices, on_device(): cover = lax.psum(partial_cover, ('rowa', 'rowb', 'col'))  126 us
    all_to_all x1, blocking collectives, on_device(): lax.all_to_all(table, 'col', split_axis=0, concat_axis=1, tiled=True)  54.6 us
    another operation x24, other arithmetic, normalize(): lower = jnp.linalg.cholesky(gram)  17.2 us
    another operation x16, other arithmetic, normalize(): jax.scipy.linalg.solve_triangular(lower, products, lower=True)  15 us
    dot_general x1, matrix products, on_device(): lax.dot_general(regrouped, regrouped, (((0,), (0,)), ((), ())), precision...  10.3 us
    dot_general x8, matrix products, on_device(): jnp.dot(vectors, cover, precision=high, preferred_element_type=jnp.float32)  8.81 us
    all_gather x1, blocking collectives, on_device(): left = lax.all_gather(images, 'col', axis=1, tiled=True)  7.1 us
  transfers between devices with their start and end apart: 1, of which 1 were waited for; matrix products, arithmetic and copies ran while one was open for 0% of the time, Pallas kernels for 0%

commit v1 on v0

--- a/solution.py
+++ b/solution.py
@@ -45,7 +45,8 @@
         precision=high,
         preferred_element_type=jnp.float32,
     )
-    cover = lax.psum(partial_cover, ("rowa", "rowb", "col"))
+    terms = lax.all_gather(partial_cover, ("rowa", "rowb", "col"))
+    cover = jnp.sum(terms, axis=0)
     previous = vectors
     lower = None
     for step in range(STEPS):

time: 276 us -> 348 us (1.26)
  waiting for transfers between devices: 127 us -> 190 us
  other arithmetic: 32.8 us -> 45.1 us
  matrix products: 26.4 us -> 22.6 us
    all_gather x0 -> x1, waiting for transfers between devices: none -> 190 us  [on_device(): terms = lax.all_gather(partial_cover, ('rowa', 'rowb', 'col'))]
    psum x1 -> x0, waiting for transfers between devices: 126 us -> none  [on_device(): cover = lax.psum(partial_cover, ('rowa', 'rowb', 'col'))]
    reduce_sum x0 -> x1, other arithmetic: none -> 12.3 us  [on_device(): cover = jnp.sum(terms, axis=0)]
    dot_general x8, matrix products: 8.81 us -> 5.07 us  [on_device(): jnp.dot(vectors, cover, precision=high, preferred_element_type=jnp.float32)]
where the time goes in v1:
time: 348 us; the launch traced here: 347 us
  waiting for transfers between devices  190 us (55%)
  blocking collectives  67.1 us (19%)
  other arithmetic  45.1 us (13%)
  matrix products  22.6 us (6%)
  between operations  14.2 us (4%)
  local copies, waits for them, and re-layouts  8.11 us (2%)
    all_gather x1, waiting for transfers between devices, on_device(): terms = lax.all_gather(partial_cover, ('rowa', 'rowb', 'col'))  190 us
    all_to_all x1, blocking collectives, on_device(): lax.all_to_all(table, 'col', split_axis=0, concat_axis=1, tiled=True)  54.5 us
    another operation x24, other arithmetic, normalize(): lower = jnp.linalg.cholesky(gram)  17.2 us
    another operation x16, other arithmetic, normalize(): jax.scipy.linalg.solve_triangular(lower, products, lower=True)  15 us
    reduce_sum x1, other arithmetic, on_device(): cover = jnp.sum(terms, axis=0)  12.3 us
    dot_general x1, matrix products, on_device(): lax.dot_general(regrouped, regrouped, (((0,), (0,)), ((), ())), precision...  10.3 us
    all_gather x1, blocking collectives, on_device(): left = lax.all_gather(images, 'col', axis=1, tiled=True)  7.17 us
  transfers between devices with their start and end apart: 1, of which 1 were waited for; matrix products, arithmetic and copies ran while one was open for 0% of the time, Pallas kernels for 0%

profile of v1, /device:TPU:0, one launch (start us, length us, event | category | flops | bytes accessed | tf_op | source)
XLA Modules:
  0.0 347.1 jit_solution(489775004383667283)
XLA Ops:
  7.2 54.5 %all_to_all.19 = f32[4,2048,128]{2,1,0:T(8,128)} all-to-all(f32[4,2048,128]{2,1,0:T(8,128)} %bitcast.128), channel_id=1, replica_groups=mesh['rowa'=2,'rowb'=4,'col'=4] {'col'}, dimensions={0} | all-to-all | bytes 8388608 | tf_op jit(solution)/shard_map/all_to_all | solution.py:38
  61.8 5.4 %copy.21 = f32[2048,4,128]{0,2,1:T(8,128)} copy(f32[2048,4,128]{2,0,1:T(8,128)} %bitcast.127) | data formatting | bytes 8388608 | tf_op jit(solution)/shard_map/all_to_all | solution.py:38
  67.1 10.3 %fusion.48 = f32[512,512]{1,0:T(8,128)} fusion(f32[2048,512]{0,1:T(8,128)} %bitcast.124), kind=kOutput, calls=%fused_computation.78 | convolution fusion | flops 6442450944 | bytes 5242880 | tf_op jit(solution)/shard_map/dot_general | solution.py:41
  77.5 5.4 %all_gather.14 = f32[16,512]{1,0:T(8,128)S(1)} all-gather(f32[16,128]{1,0:T(8,128)S(1)} %copy-done), channel_id=1, replica_groups=mesh['rowa'=2,'rowb'=4,'col'=4] {'col'}, dimensions={1}, use_global_device_ids=true | all-gather | bytes 40960 | tf_op jit(solution)/shard_map/all_gather | solution.py:40
  82.8 190.0 %all-gather.3.cloned.1.call-done = f32[16384,512]{1,0:T(8,128)} async-done(((f32[512,512]{1,0:T(8,128)}), f32[16384,512]{1,0:T(8,128)}) %all-gather.3.cloned.1.call-update) | async-done | bytes 33554448 | tf_op jit(solution)/shard_map/all_gather | solution.py:48
  272.8 12.3 %reduce_sum.9 = f32[512,512]{1,0:T(8,128)S(1)} reduce(f32[32,512,512]{2,1,0:T(8,128)} %bitcast.126, f32[]{:T(128)} %constant.45.clone.1), dimensions={0}, to_apply=%region_0.0 | reduce | flops 8126464 | bytes 34603012 | tf_op jit(solution)/shard_map/reduce_sum | solution.py:49
  286.0 1.5 cholesky.134
  288.8 1.2 custom-call.14
  291.1 1.5 cholesky.145
  293.9 1.2 custom-call.15
  296.3 1.5 cholesky.156
  299.1 1.2 custom-call.16
  301.4 1.5 cholesky.167
  304.2 1.2 custom-call.17
  306.5 1.5 cholesky.178
  309.3 1.2 custom-call.18
  311.7 1.5 cholesky.189
  314.5 1.2 custom-call.19
  316.8 1.5 cholesky.200
  319.6 1.2 custom-call.20
  321.1 4.3 %fusion.65 = f32[16,2048]{1,0:T(8,128)S(1)} fusion(f32[16,512]{1,0:T(8,128)S(1)} %fusion.12, f32[2048,512]{0,1:T(8,128)} %bitcast.125), kind=kOutput, calls=%fused_computation.95 | convolution fusion | flops 201326592 | bytes 4358144 | tf_op jit(solution)/shard_map/dot_general | solution.py:11
  326.0 7.2 %all_gather.15 = f32[16,8192]{1,0:T(8,128)S(1)} all-gather(f32[16,2048]{1,0:T(8,128)S(1)} %fusion.65), channel_id=1, replica_groups=mesh['rowa'=2,'rowb'=4,'col'=4] {'col'}, dimensions={1}, use_global_device_ids=true | all-gather | bytes 655360 | tf_op jit(solution)/shard_map/all_gather | solution.py:57
  333.4 1.5 cholesky.211
  336.2 1.2 custom-call.21
  (73 shorter events, 22.0 us)
Async XLA Ops:
  7.2 265.7 %all-gather.3.cloned.1.call-start = ((), (), s32[]{:S(2)}) async-start(), calls=%async_computation.1 | async-start | bytes 34603008 | tf_op jit(solution)/shard_map/all_gather | solution.py:48
  67.1 10.3 %copy-start = (f32[16,128]{1,0:T(8,128)S(1)}, f32[16,128]{1,0:T(8,128)}, u32[]{:S(2)}) copy-start(f32[16,128]{1,0:T(8,128)} %param.6) | copy-start | bytes 24580
Sparse Core Ops, SparseCore 0:
  77.6 195.2 all-gather.2
